TPU v7x, 32 devices: a whole 2x2x4 slice. The times are simulated.
32 devices in a mesh: rows: 8 (over y, x, core), feat: 4 (over z).
Axes of the slice: x: 2, y: 2, z: 4, core: 2. Of those that a mesh axis runs over, the one named last changes fastest.
Arguments:
- features: bfloat16 [8192, 2048], P('rows', 'feat'), may hold values from -6 to 6
- grad_out: bfloat16 [8192, 2048], P('rows', 'feat'), may hold values from -6 to 6
- eigvecs: float32 [2048, 2048], P('feat', 'rows'), may hold values from -1 to 1, as said below
- eigvals: float32 [2048], replicated, may hold values from 0.1 to 1, as said below
- whiten: bfloat16 [2048, 2048], P(None, 'feat'), may hold values from -0.125 to 0.125
Outputs:
- grad_in: bfloat16 [8192, 2048], P('rows', 'feat')
Inputs may be any that keep to these rules, and one draw needn't show every extreme that they name: `eigvecs`: the columns are orthonormal. `eigvals`: any two entries differ by at least 0.45 / 2048.
All inputs are finite; a program needn't handle non-finite values.
Results may differ from a plain program's by a relative error of at most 0.0074.
Values may be sent and summed in bfloat16 or wider, within the bound.
A program may use at most 128 MiB of HBM per device.

v0:
```python
import jax
import jax.numpy as jnp
from jax import lax
from jax.sharding import PartitionSpec as P


def divided(lam_row, lam_col, first_col):
    on_diag = (
        jnp.arange(lam_row.shape[0], dtype=jnp.int32)[:, None]
        == (first_col + jnp.arange(lam_col.shape[0], dtype=jnp.int32))[None, :]
    )
    root_row = lam_row ** (-0.5)
    root_col = lam_col ** (-0.5)
    gaps_lam = lam_row[:, None] - lam_col[None, :]
    safe_gap = jnp.where(on_diag, jnp.ones_like(gaps_lam), gaps_lam)
    off_diag = (root_row[:, None] - root_col[None, :]) / safe_gap
    diag_vals = -0.5 * lam_row[:, None] ** (-1.5) + jnp.zeros_like(gaps_lam)
    return jnp.where(on_diag, diag_vals, off_diag)


def local(features, grad_out, eigvecs, eigvals, whiten):
    highest = lax.Precision.HIGHEST
    tok_rows, own_cols = features.shape
    row_count = tok_rows * lax.axis_size("rows")
    contract_rows = (((0,), (0,)), ((), ()))
    contract_last = (((1,), (1,)), ((), ()))
    piece_x = lax.all_gather(features, "feat", axis=1, tiled=True)
    piece_g = lax.all_gather(grad_out, "feat", axis=1, tiled=True)
    left_part = lax.dot_general(
        features, piece_g, contract_rows, preferred_element_type=jnp.float32
    )
    right_part = lax.dot_general(
        grad_out, piece_x, contract_rows, preferred_element_type=jnp.float32
    )
    cross_one = left_part
    cross_two = right_part
    sum_x = jnp.sum(piece_x, axis=0, dtype=jnp.float32)
    sum_g = jnp.sum(piece_g, axis=0, dtype=jnp.float32)
    cross_one, cross_two, sum_x, sum_g = (cross_one, cross_two, sum_x, sum_g)
    cross_one, cross_two, sum_x, sum_g = lax.psum((cross_one, cross_two, sum_x, sum_g), "rows")
    both_cross = cross_one + cross_two
    col_mean = sum_x / row_count
    grad_mean = sum_g / row_count
    offset = lax.axis_index("feat") * own_cols
    mean_part = lax.dynamic_slice_in_dim(col_mean, offset, own_cols)
    grad_part = lax.dynamic_slice_in_dim(grad_mean, offset, own_cols)
    sym_gram = 0.5 * (
        both_cross
        - row_count
        * (mean_part[:, None] * grad_mean[None, :] + grad_part[:, None] * col_mean[None, :])
    )
    basis_cols = lax.all_gather(eigvecs, "feat", axis=0, tiled=True)
    basis_block = lax.all_gather(eigvecs, "rows", axis=1, tiled=True)
    narrow = basis_cols.shape[1]
    inner_prod = jnp.dot(sym_gram, basis_cols, precision=highest)
    partial_value = lax.dot_general(basis_block, inner_prod, contract_rows, precision=highest)
    rotated = lax.psum(partial_value, "feat")
    first_col = lax.axis_index("rows") * narrow
    lam_col = lax.dynamic_slice_in_dim(eigvals, first_col, narrow)
    scaled = divided(eigvals, lam_col, first_col) * rotated
    back_rot = jnp.dot(basis_block, scaled, precision=highest)
    sens_own = lax.psum_scatter(
        lax.dot_general(back_rot, basis_cols, contract_last, precision=highest),
        "rows",
        scatter_dimension=0,
        tiled=True,
    )
    scaled_own = (2.0 / row_count * sens_own).astype(jnp.bfloat16)
    sens_scaled = lax.all_gather(scaled_own, "rows", axis=0, tiled=True)
    piece_x = lax.all_gather(features, "feat", axis=1, tiled=True)
    piece_g = lax.all_gather(grad_out, "feat", axis=1, tiled=True)
    shifted = (piece_g.astype(jnp.float32) - grad_mean).astype(jnp.bfloat16)
    centered = (piece_x.astype(jnp.float32) - col_mean).astype(jnp.bfloat16)
    running = jnp.dot(shifted, whiten, preferred_element_type=jnp.float32)
    grad_in = running + lax.dot_general(
        centered, sens_scaled, contract_last, preferred_element_type=jnp.float32
    )
    return grad_in.astype(jnp.bfloat16)


def solution(mesh):
    in_specs = (P("rows", "feat"), P("rows", "feat"), P("feat", "rows"), P(), P(None, "feat"))
    out_specs = P("rows", "feat")
    return jax.shard_map(local, mesh=mesh, in_specs=in_specs, out_specs=out_specs, check_vma=False)
```

profile of v0, /device:TPU:0, one launch (start us, length us, event | category | flops | bytes accessed | tf_op | source)
XLA Modules:
  0.0 552.3 jit_solution(13871746332786428748)
XLA Ops:
  6.5 0.7 all-gather.6.cloned.1.call-update
  7.3 0.7 all-gather.8.cloned.1.call-update
  8.1 0.7 all-gather.10.cloned.1.call-update
  8.8 83.6 %all-gather.6.cloned.1.call-done = bf16[1024,2048]{1,0:T(8,128)(2,1)} async-done(((bf16[1024,512]{1,0:T(8,128)(2,1)}), bf16[1024,2048]{1,0:T(8,128)(2,1)}) %all-gather.6.cloned.1.call-update) | async-done | bytes 4194320 | tf_op jit(solution)/shard_map/all_gather | solution.py:71
  92.4 6.8 %fusion.40 = f32[512,2048]{1,0:T(8,128)} fusion(bf16[1024,512]{1,0:T(8,128)(2,1)} %param.5, bf16[1024,2048]{1,0:T(8,128)(2,1)} %all-gather.6.cloned.1.call-done), kind=kOutput, calls=%fused_computation.51 | convolution fusion | flops 2147483648 | bytes 9437184 | tf_op jit(solution)/shard_map/dot_general | solution.py:29
  99.2 74.0 %all-gather.8.cloned.1.call-done = bf16[1024,2048]{1,0:T(8,128)(2,1)} async-done(((bf16[1024,512]{1,0:T(8,128)(2,1)}), bf16[1024,2048]{1,0:T(8,128)(2,1)}) %all-gather.8.cloned.1.call-update) | async-done | bytes 4194320 | tf_op jit(solution)/shard_map/all_gather | solution.py:70
  173.2 7.8 %convolution_add_fusion = f32[512,2048]{1,0:T(8,128)} fusion(f32[512,2048]{1,0:T(8,128)} %fusion.40, bf16[1024,512]{1,0:T(8,128)(2,1)S(1)} %copy-done.3, bf16[1024,2048]{1,0:T(8,128)(2,1)} %all-gather.8.cloned.1.call-done), kind=kOutput, calls=%fused_computation.17 | convolution fusion | flops 2148532224 | bytes 13631488 | tf_op jit(solution)/shard_map/dot_general | solution.py:32
  181.1 0.5 all-gather.12.cloned.1.call-update
  181.7 3.0 convert_reduce_fusion
  185.2 0.6 convert_reduce_fusion.1
  185.8 25.6 %all-reduce = (f32[2048]{0:T(1024)S(1)}, f32[2048]{0:T(1024)S(1)}) all-reduce(f32[2048]{0:T(1024)S(1)} %convert_reduce_fusion, f32[2048]{0:T(1024)S(1)} %convert_reduce_fusion.1), channel_id=1, replica_groups=mesh['rows'=8,'feat'=4] {'rows'}, use_global_device_ids=true, to_apply=%region_3.0 | all-reduce | flops 4096 | bytes 32768 | tf_op jit(solution)/shard_map/psum | solution.py:40
  211.6 7.4 %all-gather.10.cloned.1.call-done = f32[2048,256]{1,0:T(8,128)} async-done(((f32[512,256]{1,0:T(8,128)}), f32[2048,256]{1,0:T(8,128)}) %all-gather.10.cloned.1.call-update) | async-done | bytes 2097168 | tf_op jit(solution)/shard_map/all_gather | solution.py:52
  219.0 82.8 %all-reduce.6.cloned.1.call-done = f32[512,2048]{1,0:T(8,128)} async-done(((f32[512,2048]{1,0:T(8,128)}), f32[512,2048]{1,0:T(8,128)}) %all-reduce.6.cloned.1.call-update) | async-done | bytes 4194320 | tf_op jit(solution)/shard_map/psum | solution.py:40
  301.7 6.9 %fusion.6 = f32[512,256]{1,0:T(8,128)S(1)} fusion(f32[2048,256]{1,0:T(8,128)} %all-gather.10.cloned.1.call-done, f32[512,2048]{1,0:T(8,128)} %all-reduce.6.cloned.1.call-done, f32[2048]{0:T(1024)S(1)} %get-tuple-element.11, f32[512]{0:T(512)S(1)} %dynamic_slice.11, f32[2048]{0:T(1024)S(1)} %get-tuple-element.12, f32[512]{0:T(512)S(1)} %dynamic_slice.10), kind=kOutput, calls=%fused_computation.8 | convolution fusion | flops 3227516928 | bytes 6836224 | tf_op jit(solution)/shard_map/dot_general | solution.py:55
  308.6 32.3 %all-gather.12.cloned.1.call-done = f32[512,2048]{1,0:T(8,128)} async-done(((f32[512,256]{1,0:T(8,128)}), f32[512,2048]{1,0:T(8,128)}) %all-gather.12.cloned.1.call-update) | async-done | bytes 4194320 | tf_op jit(solution)/shard_map/all_gather | solution.py:53
  340.9 10.2 %convolution_bitcast_fusion = f32[2048,256]{1,0:T(8,128)} fusion(f32[512,256]{1,0:T(8,128)S(1)} %fusion.6, f32[512,2048]{1,0:T(8,128)} %all-gather.12.cloned.1.call-done), kind=kOutput, calls=%fused_computation.18 | convolution fusion | flops 3221225472 | bytes 6815744 | tf_op jit(solution)/shard_map/dot_general | solution.py:56
  351.5 85.9 %all-reduce.4.cloned.1.call-done = f32[2048,256]{1,0:T(8,128)} async-done(((f32[2048,256]{1,0:T(8,128)}), f32[2048,256]{1,0:T(8,128)}) %all-reduce.4.cloned.1.call-update) | async-done | bytes 2097168 | tf_op jit(solution)/shard_map/psum | solution.py:57
  437.4 10.8 %fusion.15 = f32[256,512]{1,0:T(8,128)S(1)} fusion(f32[512,2048]{1,0:T(8,128)} %all-gather.12.cloned.1.call-done, f32[2048,256]{1,0:T(8,128)} %all-reduce.4.cloned.1.call-done, f32[256]{0:T(256)S(1)} %get-tuple-element.8, f32[2048]{0:T(1024)S(1)} %copy-done.5, f32[256]{0:T(256)S(1)} %get-tuple-element.7, f32[2048]{0:T(1024)S(1)} %get-tuple-element.10, ...), kind=kOutput, calls=%fused_computation.20 | convolution fusion | flops 3224895488 | bytes 6843392 | tf_op jit(solution)/shard_map/dot_general | solution.py:61
  448.2 8.4 %fusion.41 = f32[512,2048]{1,0:T(8,128)} fusion(f32[256,512]{1,0:T(8,128)S(1)} %fusion.15, f32[2048,256]{1,0:T(8,128)S(1)} %copy-done.4), kind=kOutput, calls=%fused_computation.52 | convolution fusion | flops 3221225472 | bytes 6815744 | tf_op jit(solution)/shard_map/dot_general | solution.py:63
  457.0 50.0 %reduce-scatter.2.cloned.1.call-done = f32[64,2048]{1,0:T(8,128)} async-done(((f32[512,2048]{1,0:T(8,128)}), f32[64,2048]{1,0:T(8,128)}) %reduce-scatter.2.cloned.1.call-update) | async-done | bytes 524304 | tf_op jit(solution)/shard_map/reduce_scatter | solution.py:62
  507.0 1.8 multiply_convert_fusion
  508.8 27.9 %all-gather.14.cloned.1.call-done = bf16[512,2048]{1,0:T(8,128)(2,1)} async-done(((bf16[64,2048]{1,0:T(8,128)(2,1)}), bf16[512,2048]{1,0:T(8,128)(2,1)}) %all-gather.14.cloned.1.call-update) | async-done | bytes 2097168 | tf_op jit(solution)/shard_map/all_gather | solution.py:69
  536.7 5.4 fusion.2
  542.1 3.3 add_convert_fusion
  (30 shorter events, 1.6 us)
Async XLA Ops:
  6.5 535.6 %copy-start = (bf16[2048,512]{1,0:T(8,128)(2,1)S(1)}, bf16[2048,512]{1,0:T(8,128)(2,1)}, u32[]{:S(2)}) copy-start(bf16[2048,512]{1,0:T(8,128)(2,1)} %param.9) | copy-start | bytes 6291460
  6.5 85.9 %all-gather.6.cloned.1.call-start = ((), (), s32[]{:S(2)}) async-start(), calls=%async_computation.1 | async-start | bytes 5242880 | tf_op jit(solution)/shard_map/all_gather | solution.py:71
  7.3 166.0 %all-gather.8.cloned.1.call-start = ((), (), s32[]{:S(2)}) async-start(), calls=%async_computation.2 | async-start | bytes 5242880 | tf_op jit(solution)/shard_map/all_gather | solution.py:70
  8.0 211.0 %all-gather.10.cloned.1.call-start = ((), (), s32[]{:S(2)}) async-start(), calls=%async_computation.3 | async-start | bytes 2621440 | tf_op jit(solution)/shard_map/all_gather | solution.py:52
  8.7 164.5 %copy-start.3 = (bf16[1024,512]{1,0:T(8,128)(2,1)S(1)}, bf16[1024,512]{1,0:T(8,128)(2,1)}, u32[]{:S(2)}) copy-start(bf16[1024,512]{1,0:T(8,128)(2,1)} %param.6) | copy-start | bytes 3145732
  8.8 293.0 %all-reduce.6.cloned.1.call-start = ((), (), s32[]{:S(2)}) async-start(), calls=%async_computation.8 | async-start | bytes 8388608 | tf_op jit(solution)/shard_map/psum | solution.py:40
  181.1 159.9 %all-gather.12.cloned.1.call-start = ((), (), s32[]{:S(2)}) async-start(), calls=%async_computation.4 | async-start | bytes 4718592 | tf_op jit(solution)/shard_map/all_gather | solution.py:53
  181.7 255.8 %all-reduce.4.cloned.1.call-start = ((), (), s32[]{:S(2)}) async-start(), calls=%async_computation.5 | async-start | bytes 4194304 | tf_op jit(solution)/shard_map/psum | solution.py:57
  181.7 3.5 copy-start.1
  308.6 42.8 %copy-start.5 = (f32[2048]{0:T(1024)S(1)}, f32[2048]{0:T(1024)}, u32[]{:S(2)}) copy-start(f32[2048]{0:T(1024)} %param.8) | copy-start | bytes 24580
  351.1 155.9 %reduce-scatter.2.cloned.1.call-start = ((), (), s32[]{:S(2)}) async-start(), calls=%async_computation.6 | async-start | bytes 4718592 | tf_op jit(solution)/shard_map/reduce_scatter | solution.py:62
  437.4 10.8 %copy-start.4 = (f32[2048,256]{1,0:T(8,128)S(1)}, f32[2048,256]{1,0:T(8,128)}, u32[]{:S(2)}) copy-start(f32[2048,256]{1,0:T(8,128)} %all-gather.10.cloned.1.call-done) | copy-start | bytes 6291460
  456.7 80.1 %all-gather.14.cloned.1.call-start = ((), (), s32[]{:S(2)}) async-start(), calls=%async_computation.7 | async-start | bytes 2359296 | tf_op jit(solution)/shard_map/all_gather | solution.py:69
  536.7 5.4 copy-start.2
Sparse Core Ops, SparseCore 0:
  8.9 83.4 all-gather.5
  94.0 79.2 all-gather.7
  174.8 44.1 all-gather.9
  222.1 79.5 all-reduce.5
  303.5 37.3 all-gather.11
  351.3 86.1 all-reduce.3
  456.8 50.1 reduce-scatter.1
  508.9 27.7 all-gather.13
where the time goes:
time: 552 us
  waiting for transfers between devices  447 us (81%)
  matrix products  59.6 us (11%)
  blocking collectives  25.6 us (5%)
  between operations  13.6 us (2%)
    psum x1, waiting for transfers between devices, local(): rotated = lax.psum(partial_value, 'feat')  85.9 us
    all_gather x1, waiting for transfers between devices, local(): piece_g = lax.all_gather(grad_out, 'feat', axis=1, tiled=True)  83.6 us
    psum x1, waiting for transfers between devices, local(): lax.psum((cross_one, cross_two, sum_x, sum_g), 'rows')  82.8 us
    all_gather x1, waiting for transfers between devices, local(): piece_x = lax.all_gather(features, 'feat', axis=1, tiled=True)  74 us
    reduce_scatter x1, waiting for transfers between devices, local(): lax.psum_scatter(lax.dot_general(back_rot, basis_cols, contract_last, pre...  50 us
    all_gather x1, waiting for transfers between devices, local(): basis_block = lax.all_gather(eigvecs, 'rows', axis=1, tiled=True)  32.3 us
    all_gather x1, waiting for transfers between devices, local(): sens_scaled = lax.all_gather(scaled_own, 'rows', axis=0, tiled=True)  27.9 us
    psum x1, blocking collectives, local(): lax.psum((cross_one, cross_two, sum_x, sum_g), 'rows')  25.6 us
  transfers between devices with their start and end apart: 8, of which 8 were waited for; matrix products, arithmetic and copies ran while one was open for 5% of the time, Pallas kernels for 0%

commit v1 on v0

--- a/solution.py
+++ b/solution.py
@@ -54,7 +54,7 @@
     narrow = basis_cols.shape[1]
     inner_prod = jnp.dot(sym_gram, basis_cols, precision=highest)
     partial_value = lax.dot_general(basis_block, inner_prod, contract_rows, precision=highest)
-    rotated = lax.psum(partial_value, "feat")
+    rotated = jnp.sum(lax.all_gather(partial_value, "feat"), axis=0)
     first_col = lax.axis_index("rows") * narrow
     lam_col = lax.dynamic_slice_in_dim(eigvals, first_col, narrow)
     scaled = divided(eigvals, lam_col, first_col) * rotated

time: 552 us -> 630 us (1.14)
  waiting for transfers between devices: 447 us -> 510 us
  local copies, waits for them, and re-layouts: 0.75 us -> 11.6 us
  other arithmetic: 5.43 us -> 15.4 us
    all_gather x0 -> x1, waiting for transfers between devices: none -> 150 us  [local(): rotated = jnp.sum(lax.all_gather(partial_value, 'feat'), axis=0)]
    psum x1 -> x0, waiting for transfers between devices: 85.9 us -> none  [local(): rotated = lax.psum(partial_value, 'feat')]
    all_gather x0 -> x1, local copies, waits for them, and re-layouts: none -> 10.8 us  [local(): rotated = jnp.sum(lax.all_gather(partial_value, 'feat'), axis=0)]
    reduce_sum x0 -> x1, other arithmetic: none -> 9.98 us  [local(): rotated = jnp.sum(lax.all_gather(partial_value, 'feat'), axis=0)]
  transfers between devices with their start and end apart: 8 -> 8, of which waited for: 8 -> 8; matrix products, arithmetic and copies ran while one was open for 5% -> 4% of each run, Pallas kernels for 0% -> 0%
where the time goes in v1:
time: 630 us
  waiting for transfers between devices  510 us (81%)
  matrix products  53.6 us (9%)
  blocking collectives  25.6 us (4%)
  other arithmetic  15.4 us (2%)
  between operations  13.6 us (2%)
  local copies, waits for them, and re-layouts  11.6 us (2%)
    all_gather x1, waiting for transfers between devices, local(): rotated = jnp.sum(lax.all_gather(partial_value, 'feat'), axis=0)  150 us
    all_gather x1, waiting for transfers between devices, local(): piece_g = lax.all_gather(grad_out, 'feat', axis=1, tiled=True)  83.6 us
    psum x1, waiting for transfers between devices, local(): lax.psum((cross_one, cross_two, sum_x, sum_g), 'rows')  82.8 us
    all_gather x1, waiting for transfers between devices, local(): piece_x = lax.all_gather(features, 'feat', axis=1, tiled=True)  74 us
    reduce_scatter x1, waiting for transfers between devices, local(): lax.psum_scatter(lax.dot_general(back_rot, basis_cols, contract_last, pre...  49.5 us
    all_gather x1, waiting for transfers between devices, local(): basis_block = lax.all_gather(eigvecs, 'rows', axis=1, tiled=True)  32.3 us
    all_gather x1, waiting for transfers between devices, local(): sens_scaled = lax.all_gather(scaled_own, 'rows', axis=0, tiled=True)  27.9 us
    psum x1, blocking collectives, local(): lax.psum((cross_one, cross_two, sum_x, sum_g), 'rows')  25.6 us
  transfers between devices with their start and end apart: 8, of which 8 were waited for; matrix products, arithmetic and copies ran while one was open for 4% of the time, Pallas kernels for 0%

profile of v1, /device:TPU:0, one launch (start us, length us, event | category | flops | bytes accessed | tf_op | source)
XLA Modules:
  0.0 629.7 jit_solution(17155769543071064466)
XLA Ops:
  6.5 0.7 all-gather.8.cloned.1.call-update
  7.3 0.7 all-gather.10.cloned.1.call-update
  8.1 0.7 all-gather.12.cloned.1.call-update
  8.8 83.6 %all-gather.8.cloned.1.call-done = bf16[1024,2048]{1,0:T(8,128)(2,1)} async-done(((bf16[1024,512]{1,0:T(8,128)(2,1)}), bf16[1024,2048]{1,0:T(8,128)(2,1)}) %all-gather.8.cloned.1.call-update) | async-done | bytes 4194320 | tf_op jit(solution)/shard_map/all_gather | solution.py:71
  92.4 6.9 %fusion.40 = f32[512,2048]{1,0:T(8,128)} fusion(bf16[1024,512]{1,0:T(8,128)(2,1)} %param.5, bf16[1024,2048]{1,0:T(8,128)(2,1)} %all-gather.8.cloned.1.call-done), kind=kOutput, calls=%fused_computation.51 | convolution fusion | flops 2147483648 | bytes 9437184 | tf_op jit(solution)/shard_map/dot_general | solution.py:29
  99.3 74.0 %all-gather.10.cloned.1.call-done = bf16[1024,2048]{1,0:T(8,128)(2,1)} async-done(((bf16[1024,512]{1,0:T(8,128)(2,1)}), bf16[1024,2048]{1,0:T(8,128)(2,1)}) %all-gather.10.cloned.1.call-update) | async-done | bytes 4194320 | tf_op jit(solution)/shard_map/all_gather | solution.py:70
  173.2 7.8 %convolution_add_fusion = f32[512,2048]{1,0:T(8,128)} fusion(f32[512,2048]{1,0:T(8,128)} %fusion.40, bf16[1024,512]{1,0:T(8,128)(2,1)S(1)} %copy-done.3, bf16[1024,2048]{1,0:T(8,128)(2,1)} %all-gather.10.cloned.1.call-done), kind=kOutput, calls=%fused_computation.17 | convolution fusion | flops 2148532224 | bytes 13631488 | tf_op jit(solution)/shard_map/dot_general | solution.py:32
  181.7 3.0 convert_reduce_fusion
  185.9 25.6 %all-reduce = (f32[2048]{0:T(1024)S(1)}, f32[2048]{0:T(1024)S(1)}) all-reduce(f32[2048]{0:T(1024)S(1)} %convert_reduce_fusion, f32[2048]{0:T(1024)S(1)} %convert_reduce_fusion.1), channel_id=1, replica_groups=mesh['rows'=8,'feat'=4] {'rows'}, use_global_device_ids=true, to_apply=%region_3.0 | all-reduce | flops 4096 | bytes 32768 | tf_op jit(solution)/shard_map/psum | solution.py:40
  211.6 7.4 %all-gather.12.cloned.1.call-done = f32[2048,256]{1,0:T(8,128)} async-done(((f32[512,256]{1,0:T(8,128)}), f32[2048,256]{1,0:T(8,128)}) %all-gather.12.cloned.1.call-update) | async-done | bytes 2097168 | tf_op jit(solution)/shard_map/all_gather | solution.py:52
  219.0 82.8 %all-reduce.3.cloned.1.call-done = f32[512,2048]{1,0:T(8,128)} async-done(((f32[512,2048]{1,0:T(8,128)}), f32[512,2048]{1,0:T(8,128)}) %all-reduce.3.cloned.1.call-update) | async-done | bytes 4194320 | tf_op jit(solution)/shard_map/psum | solution.py:40
  301.7 6.9 %fusion.6 = f32[512,256]{1,0:T(8,128)S(1)} fusion(f32[2048,256]{1,0:T(8,128)} %all-gather.12.cloned.1.call-done, f32[512,2048]{1,0:T(8,128)} %all-reduce.3.cloned.1.call-done, f32[2048]{0:T(1024)S(1)} %get-tuple-element.11, f32[512]{0:T(512)S(1)} %dynamic_slice.11, f32[2048]{0:T(1024)S(1)} %get-tuple-element.12, f32[512]{0:T(512)S(1)} %dynamic_slice.10), kind=kOutput, calls=%fused_computation.8 | convolution fusion | flops 3227516928 | bytes 6836224 | tf_op jit(solution)/shard_map/dot_general | solution.py:55
  308.6 32.3 %all-gather.14.cloned.1.call-done = f32[512,2048]{1,0:T(8,128)} async-done(((f32[512,256]{1,0:T(8,128)}), f32[512,2048]{1,0:T(8,128)}) %all-gather.14.cloned.1.call-update) | async-done | bytes 4194320 | tf_op jit(solution)/shard_map/all_gather | solution.py:53
  340.9 7.2 %convolution_bitcast_fusion = f32[2048,256]{0,1:T(8,128)} fusion(f32[512,256]{1,0:T(8,128)S(1)} %fusion.6, f32[512,2048]{1,0:T(8,128)} %all-gather.14.cloned.1.call-done), kind=kOutput, calls=%fused_computation.18 | convolution fusion | flops 3221225472 | bytes 6815744 | tf_op jit(solution)/shard_map/dot_general | solution.py:56
  348.3 149.6 %all-gather.18.cloned.1.call-done = f32[8192,256]{0,1:T(8,128)} async-done(((f32[2048,256]{0,1:T(8,128)}), f32[8192,256]{0,1:T(8,128)}) %all-gather.18.cloned.1.call-update) | async-done | bytes 8388624 | tf_op jit(solution)/shard_map/all_gather | solution.py:57
  497.9 10.8 %reshape.15 = f32[4,2048,256]{1,0,2:T(4,128)} reshape(f32[8192,256]{0,1:T(8,128)} %all-gather.18.cloned.1.call-done) | data formatting | bytes 16777216 | tf_op jit(solution)/shard_map/all_gather | solution.py:57
  508.7 10.0 %reduce_sum.29 = f32[2048,256]{0,1:T(8,128)} reduce(f32[4,2048,256]{1,0,2:T(4,128)} %reshape.15, f32[]{:T(128)} %constant.15.clone.1), dimensions={0}, to_apply=%region_6.0 | reduce | flops 1572864 | bytes 10485764 | tf_op jit(solution)/shard_map/reduce_sum | solution.py:57
  518.7 7.6 %fusion.15 = f32[256,512]{1,0:T(8,128)S(1)} fusion(f32[512,2048]{1,0:T(8,128)} %all-gather.14.cloned.1.call-done, f32[2048,256]{0,1:T(8,128)} %reduce_sum.29, f32[256]{0:T(256)S(1)} %get-tuple-element.8, f32[2048]{0:T(1024)S(1)} %copy-done.5, f32[256]{0:T(256)S(1)} %get-tuple-element.7, f32[2048]{0:T(1024)S(1)} %get-tuple-element.10, ...), kind=kOutput, calls=%fused_computation.20 | convolution fusion | flops 3224895488 | bytes 6843392 | tf_op jit(solution)/shard_map/dot_general | solution.py:61
  526.3 8.6 %fusion.41 = f32[512,2048]{1,0:T(8,128)} fusion(f32[256,512]{1,0:T(8,128)S(1)} %fusion.15, f32[2048,256]{1,0:T(8,128)S(1)} %copy-done.4), kind=kOutput, calls=%fused_computation.52 | convolution fusion | flops 3221225472 | bytes 6815744 | tf_op jit(solution)/shard_map/dot_general | solution.py:63
  534.9 49.5 %reduce-scatter.2.cloned.1.call-done = f32[64,2048]{1,0:T(8,128)} async-done(((f32[512,2048]{1,0:T(8,128)}), f32[64,2048]{1,0:T(8,128)}) %reduce-scatter.2.cloned.1.call-update) | async-done | bytes 524304 | tf_op jit(solution)/shard_map/reduce_scatter | solution.py:62
  584.4 1.8 multiply_convert_fusion
  586.2 27.9 %all-gather.16.cloned.1.call-done = bf16[512,2048]{1,0:T(8,128)(2,1)} async-done(((bf16[64,2048]{1,0:T(8,128)(2,1)}), bf16[512,2048]{1,0:T(8,128)(2,1)}) %all-gather.16.cloned.1.call-update) | async-done | bytes 2097168 | tf_op jit(solution)/shard_map/all_gather | solution.py:69
  614.1 5.4 fusion.2
  619.5 3.3 add_convert_fusion
  (32 shorter events, 2.3 us)
Async XLA Ops:
  6.5 613.0 %copy-start = (bf16[2048,512]{1,0:T(8,128)(2,1)S(1)}, bf16[2048,512]{1,0:T(8,128)(2,1)}, u32[]{:S(2)}) copy-start(bf16[2048,512]{1,0:T(8,128)(2,1)} %param.9) | copy-start | bytes 6291460
  6.5 85.9 %all-gather.8.cloned.1.call-start = ((), (), s32[]{:S(2)}) async-start(), calls=%async_computation.1 | async-start | bytes 5242880 | tf_op jit(solution)/shard_map/all_gather | solution.py:71
  7.3 166.0 %all-gather.10.cloned.1.call-start = ((), (), s32[]{:S(2)}) async-start(), calls=%async_computation.2 | async-start | bytes 5242880 | tf_op jit(solution)/shard_map/all_gather | solution.py:70
  8.0 211.0 %all-gather.12.cloned.1.call-start = ((), (), s32[]{:S(2)}) async-start(), calls=%async_computation.3 | async-start | bytes 2621440 | tf_op jit(solution)/shard_map/all_gather | solution.py:52
  8.7 164.5 %copy-start.3 = (bf16[1024,512]{1,0:T(8,128)(2,1)S(1)}, bf16[1024,512]{1,0:T(8,128)(2,1)}, u32[]{:S(2)}) copy-start(bf16[1024,512]{1,0:T(8,128)(2,1)} %param.6) | copy-start | bytes 3145732
  8.8 293.0 %all-reduce.3.cloned.1.call-start = ((), (), s32[]{:S(2)}) async-start(), calls=%async_computation.8 | async-start | bytes 8388608 | tf_op jit(solution)/shard_map/psum | solution.py:40
  181.1 159.8 %all-gather.14.cloned.1.call-start = ((), (), s32[]{:S(2)}) async-start(), calls=%async_computation.4 | async-start | bytes 4718592 | tf_op jit(solution)/shard_map/all_gather | solution.py:53
  181.7 316.2 %all-gather.18.cloned.1.call-start = ((), (), s32[]{:S(2)}) async-start(), calls=%async_computation.7 | async-start | bytes 10485760 | tf_op jit(solution)/shard_map/all_gather | solution.py:57
  181.7 3.5 copy-start.1
  308.6 39.6 %copy-start.5 = (f32[2048]{0:T(1024)S(1)}, f32[2048]{0:T(1024)}, u32[]{:S(2)}) copy-start(f32[2048]{0:T(1024)} %param.8) | copy-start | bytes 24580
  348.1 236.3 %reduce-scatter.2.cloned.1.call-start = ((), (), s32[]{:S(2)}) async-start(), calls=%async_computation.5 | async-start | bytes 4718592 | tf_op jit(solution)/shard_map/reduce_scatter | solution.py:62
  518.7 7.6 %copy-start.4 = (f32[2048,256]{1,0:T(8,128)S(1)}, f32[2048,256]{1,0:T(8,128)}, u32[]{:S(2)}) copy-start(f32[2048,256]{1,0:T(8,128)} %all-gather.12.cloned.1.call-done) | copy-start | bytes 6291460
  534.9 79.2 %all-gather.16.cloned.1.call-start = ((), (), s32[]{:S(2)}) async-start(), calls=%async_computation.6 | async-start | bytes 2359296 | tf_op jit(solution)/shard_map/all_gather | solution.py:69
  614.1 5.4 copy-start.2
Sparse Core Ops, SparseCore 0:
  8.9 83.4 all-gather.7
  94.0 79.2 all-gather.9
  174.8 44.1 all-gather.11
  222.1 79.5 all-reduce.2
  303.5 37.3 all-gather.13
  348.3 149.5 all-gather.17
  535.0 49.3 reduce-scatter.1
  586.3 27.7 all-gather.15
